TPU v7x, 128 devices: a whole 4x4x4 slice. The times are simulated.
128 devices in a mesh: shot: 16 (over y, z), rcv: 8 (over x, core).
Axes of the slice: x: 4, y: 4, z: 4, core: 2. Of those that a mesh axis runs over, the one named last changes fastest.
Arguments:
- shot_data: bfloat16 [512, 2048, 256], P('shot', 'rcv'), may hold values from -0.25 to 0.25
- code: int32 [32, 512], P(None, 'shot'), may hold values from -1 to 1, as said below
- observed: bfloat16 [32, 2048, 256], P('shot', 'rcv'), may hold values from -6 to 6
- block_of: int32 [2048, 1], replicated, may hold values from 0 to 7; in each aligned block of 256 rows (0 to 255, 256 to 511, ...) at most 64 rows name the same one
- stencil_index: int32 [2048, 4], replicated, may hold values from 0 to 255
- stencil_weight: float32 [2048, 4], replicated, may hold values from -0.5 to 1
Outputs:
- adjoint_source: float32 [32, 2048, 256], P('shot', 'rcv')
Inputs may be any that keep to these rules, and one draw needn't show every extreme that they name: `code`: every entry is -1 or 1. `block_of`: among the receivers of one index of rcv (aligned blocks of 256 rows) at most 64 map to one model block.
All inputs are finite; a program needn't handle non-finite values.
Results may differ from a plain program's by a relative error of at most 0.0038.
Values may be sent and summed in bfloat16 or wider, within the bound.
A program may use at most 64 MiB of HBM per device.

v0:
```python
import jax.numpy as jnp
from jax import lax

SUPERS = 32
GRID = 256
STENCIL = 4
BLOCKS = 8


def spread_weights(stencil_index, stencil_weight):
    receivers = stencil_index.shape[0]
    points = jnp.arange(GRID, dtype=jnp.int32)[:, None]
    spread = jnp.zeros((GRID, receivers), jnp.float32)
    for which in range(STENCIL):
        spread = spread + jnp.where(
            points == stencil_index[:, which][None, :], stencil_weight[:, which][None, :], 0.0
        )
    return spread


def reference(shot_data, code, observed, block_of, stencil_index, stencil_weight):
    shots, receivers, samples = shot_data.shape
    flat_rows = shot_data.reshape(shots, receivers * samples)
    supershot = jnp.dot(code.astype(jnp.bfloat16), flat_rows, preferred_element_type=jnp.float32)
    supershot = supershot.reshape(SUPERS, receivers, samples)
    residual = (supershot - observed.astype(jnp.float32)).astype(jnp.bfloat16)
    spread = spread_weights(stencil_index, stencil_weight)
    block_ids = jnp.arange(BLOCKS, dtype=jnp.int32)[:, None, None]
    injection = jnp.where(block_ids == block_of[:, 0][None, None, :], spread[None], 0.0)
    injection = injection.reshape(BLOCKS * GRID, receivers).astype(jnp.bfloat16)
    return jnp.einsum(
        "cr,krt->kct",
        injection.astype(jnp.float32),
        residual.astype(jnp.float32),
        precision=lax.Precision.HIGHEST,
    )


def solution(mesh):
    return reference
```

profile of v0, /device:TPU:1, one launch (start us, length us, event | category | flops | bytes accessed | tf_op | source)
XLA Modules:
  0.0 152.9 jit_solution(15032212178310516860)
XLA Ops:
  6.5 0.0 reduce-scatter.4.cloned.1.call-start
  6.5 8.0 %fusion = f32[32,256,256]{2,0,1:T(8,128)} fusion(s32[32,32]{1,0:T(8,128)} %param, bf16[4,8,256,256]{3,2,1,0:T(8,128)(2,1)} %bitcast.38), kind=kOutput, calls=%fused_computation | convolution fusion | flops 134218752 | bytes 12587008 | tf_op jit(solution)/dot_general | solution.py:24
  14.6 9.9 %copy.3 = f32[32,256,256]{1,2,0:T(8,128)} copy(f32[32,256,256]{2,0,1:T(8,128)} %fusion) | data formatting | bytes 16777216 | tf_op jit(solution)/dot_general | solution.py:24
  24.5 0.0 copy-start
  24.5 0.0 copy-start.4
  24.5 0.0 copy-start.3
  24.5 0.0 copy-start.1
  24.5 0.0 copy-start.2
  24.5 0.0 reduce-scatter.4.cloned.1.call-update
  24.6 0.0 all-gather.4.cloned.1.call-start
  24.6 0.8 copy-done
  25.5 0.1 copy
  25.6 86.8 %reduce-scatter.4.cloned.1.call-done = f32[2,256,256]{1,2,0:T(8,128)} async-done(((f32[32,256,256]{1,2,0:T(8,128)}), f32[2,256,256]{1,2,0:T(8,128)}) %reduce-scatter.4.cloned.1.call-update) | async-done | bytes 524304
  112.4 1.8 %subtract_convert_fusion = bf16[2,256,256]{1,2,0:T(8,128)(2,1)} fusion(f32[2,256,256]{1,2,0:T(8,128)} %reduce-scatter.4.cloned.1.call-done, bf16[2,256,256]{1,2,0:T(8,128)(2,1)S(1)} %copy), kind=kLoop, calls=%fused_computation.22 | loop fusion | flops 393216 | bytes 1048576 | tf_op jit(solution)/convert_element_type | solution.py:26
  114.2 0.0 all-gather.4.cloned.1.call-update
  114.2 0.0 copy-done.4
  114.2 0.7 dynamic-slice.5
  114.9 0.0 copy-done.3
  114.9 0.7 compare_reduce_fusion
  115.6 0.0 copy-done.1
  115.6 0.0 copy-done.2
  115.7 26.5 %all-gather.4.cloned.1.call-done = bf16[2,2048,256]{1,2,0:T(8,128)(2,1)} async-done(((bf16[2,256,256]{1,2,0:T(8,128)(2,1)}), bf16[2,2048,256]{1,2,0:T(8,128)(2,1)}) %all-gather.4.cloned.1.call-update) | async-done | bytes 2097168 | tf_op jit(solution)/convert_element_type | solution.py:26
  142.2 2.9 %convolution_bitcast_fusion = f32[2,256,256]{1,2,0:T(8,128)S(1)} fusion(bf16[2,2048,256]{1,2,0:T(8,128)(2,1)} %all-gather.4.cloned.1.call-done, f32[2048]{0:T(1024)S(1)} %bitcast.40, s32[2048]{0:T(1024)S(1)} %bitcast.44, f32[2048]{0:T(1024)S(1)} %bitcast.41, s32[2048]{0:T(1024)S(1)} %bitcast.45, f32[2048]{0:T(1024)S(1)} %bitcast.42, s32[2048]{0:T(1024)S(1)} %bitcast.46, ...), kind=kOutput, calls=%fused_computation.9 | convolution fusion | flops 543686656 | bytes 2689024 | tf_op jit(solution)/cr,krt->kct/dot_general | solution.py:31
  145.1 1.0 copy.1
  (2 shorter events, 0.1 us)
Async XLA Ops:
  6.5 105.9 %reduce-scatter.4.cloned.1.call-start = ((), (), s32[]{:S(2)}) async-start(), calls=%async_computation.2 | async-start | bytes 8912896
  24.5 0.9 copy-start
  24.5 89.7 %copy-start.4 = (s32[128]{0:T(128)S(1)}, s32[128]{0:T(128)}, u32[]{:S(2)}) copy-start(s32[128]{0:T(128)} %constant.13) | copy-start | bytes 1540
  24.5 90.4 %copy-start.3 = (s32[2048,1]{0,1:T(1,128)S(1)}, s32[2048,1]{0,1:T(1,128)}, u32[]{:S(2)}) copy-start(s32[2048,1]{0,1:T(1,128)} %param.3) | copy-start | bytes 24580
  24.5 91.1 %copy-start.1 = (f32[2048,4]{0,1:T(4,128)S(1)}, f32[2048,4]{0,1:T(4,128)}, u32[]{:S(2)}) copy-start(f32[2048,4]{0,1:T(4,128)} %param.5) | copy-start | bytes 98308
  24.5 91.1 %copy-start.2 = (s32[2048,4]{0,1:T(4,128)S(1)}, s32[2048,4]{0,1:T(4,128)}, u32[]{:S(2)}) copy-start(s32[2048,4]{0,1:T(4,128)} %param.4) | copy-start | bytes 98308
  24.6 117.6 %all-gather.4.cloned.1.call-start = ((), (), s32[]{:S(2)}) async-start(), calls=%async_computation.1 | async-start | bytes 2359296 | tf_op jit(solution)/convert_element_type | solution.py:26
Sparse Core Ops, SparseCore 0:
  24.7 87.6 reduce-scatter.3
  114.3 27.7 all-gather.3
where the time goes:
time: 153 us
  waiting for transfers between devices  113 us (74%)
  between operations  13.5 us (9%)
  local copies, waits for them, and re-layouts  12.6 us (8%)
  matrix products  10.9 us (7%)
  other arithmetic  2.51 us (2%)
    unnamed x3, waiting for transfers between devices  86.8 us
    convert_element_type x1, waiting for transfers between devices, reference(): residual = (supershot - observed.astype(jnp.float32)).astype(jnp.bfloat16)  26.5 us
    dot_general x1, local copies, waits for them, and re-layouts, reference(): jnp.dot(code.astype(jnp.bfloat16), flat_rows, preferred_element_type=jnp....  9.94 us
    dot_general x1, matrix products, reference(): jnp.dot(code.astype(jnp.bfloat16), flat_rows, preferred_element_type=jnp....  8.03 us
  transfers between devices with their start and end apart: 2, of which 2 were waited for; matrix products, arithmetic and copies ran while one was open for 1% of the time, Pallas kernels for 0%

commit v1 on v0

v1 whole, which is shorter than its diff:
```python
import jax
import jax.numpy as jnp
from jax import lax
from jax.experimental import pallas as pl
from jax.experimental.pallas import tpu as pltpu
from jax.sharding import PartitionSpec as P

SUPERS = 32
GRID = 256
STENCIL = 4
BLOCKS = 8
CAP = 64
RING = 4
RCV = 256
HALF = RCV // 2
SAMPLES = 256
LANES = 128
SHOTS_DEV = 32
GROUP = 16
ROWS = SUPERS * GROUP
DEPTH = SHOTS_DEV * GROUP
ORDER = (2, 1, 3, 0)
F32, BF16, I32 = jnp.float32, jnp.bfloat16, jnp.int32
MESH = pl.DeviceIdType.MESH


def iota(shape, dim):
    return lax.broadcasted_iota(I32, shape, dim)


def encoding_rows(shape, y, z):
    row = iota(shape, 0)
    kk = row // (ROWS // 2)
    first = (row // (4 * GROUP)) % 4
    spot = (row // GROUP) % 4
    second = jnp.where(spot == 0, 2, jnp.where(spot == 1, 1, jnp.where(spot == 2, 3, 0)))
    dy = jnp.where(kk == 0, first, second)
    dz = jnp.where(kk == 0, second, first)
    return 8 * ((y + dy) % 4) + 2 * ((z + dz) % 4) + kk


def kernel(
    shot_hbm, code_hbm, obs_hbm, blk_hbm, idx_hbm, wgt_hbm, out_hbm,
    xbuf, codebuf, obsbuf, blk, idx, wgt, enc, inj, injc, sel, obuf,
    own, keep, send1, recv1, send2, recv2, send3, recv3,
    load_sem, out_sem, s1_sem, r1_sem, s2_sem, r2_sem, s3_sem, r3_sem,
):
    shot, rcv = lax.axis_index("shot"), lax.axis_index("rcv")
    y, z = shot // 4, shot % 4

    def at_shot(dy, dz):
        return (((y + dy) % 4) * 4 + (z + dz) % 4, rcv)

    def neighbour(kk, stage, direction):
        step = 1 if direction == 0 else 3
        along_y = (kk == 0) == (stage == 1)
        return at_shot(step, 0) if along_y else at_shot(0, step)

    loads = [pltpu.make_async_copy(code_hbm, codebuf, load_sem.at[0])]
    for chunk in range(4):
        rows = pl.ds(chunk * 64, 64)
        loads.append(pltpu.make_async_copy(shot_hbm.at[:, rows], xbuf.at[:, rows], load_sem.at[1 + chunk]))
    loads.append(pltpu.make_async_copy(obs_hbm, obsbuf, load_sem.at[5]))
    loads.append(pltpu.make_async_copy(blk_hbm, blk, load_sem.at[6]))
    loads.append(pltpu.make_async_copy(idx_hbm, idx, load_sem.at[7]))
    loads.append(pltpu.make_async_copy(wgt_hbm, wgt, load_sem.at[8]))
    for load in loads:
        load.start()

    barrier = pltpu.get_barrier_semaphore()
    for peer in (at_shot(1, 0), at_shot(3, 0), at_shot(0, 1), at_shot(0, 3)):
        pl.semaphore_signal(barrier, inc=1, device_id=peer, device_id_type=MESH)
    for off in range(1, BLOCKS):
        pl.semaphore_signal(barrier, inc=1, device_id=(shot, (rcv + off) % BLOCKS), device_id_type=MESH)

    loads[0].wait()
    pick = (encoding_rows((ROWS, SUPERS), y, z) == iota((ROWS, SUPERS), 1)).astype(BF16)
    codes = jnp.dot(pick, codebuf[...].astype(F32).astype(BF16), preferred_element_type=F32).astype(BF16)
    widen = (iota((SHOTS_DEV, DEPTH), 1) // GROUP == iota((SHOTS_DEV, DEPTH), 0)).astype(BF16)
    wide = jnp.dot(codes, widen, preferred_element_type=F32)
    same = iota((ROWS, DEPTH), 0) % GROUP == iota((ROWS, DEPTH), 1) % GROUP
    enc[...] = jnp.where(same, wide, 0.0).astype(BF16)

    def half_rows(half):
        return pl.ds(half * HALF, HALF)

    def encode(half, chunk):
        def body(step, carry):
            r0 = pl.multiple_of(chunk * 64 + step * GROUP, GROUP)
            data = xbuf[:, pl.ds(r0, GROUP), :].reshape(DEPTH, SAMPLES)
            for kk in range(2):
                product = jnp.dot(enc[kk * 256:(kk + 1) * 256, :], data, preferred_element_type=F32)
                product = product.reshape(4, 4, GROUP, SAMPLES)
                for th in range(2):
                    part = product[:, :, :, th * LANES:(th + 1) * LANES]
                    rows = pl.ds(r0, GROUP)
                    inner = pl.ds(pl.multiple_of(r0 - half * HALF, GROUP), GROUP)
                    own[kk, th, :, rows, :] = part[0]
                    send1[kk, th, 1, :, rows, :] = part[2].astype(BF16)
                    if half == 0:
                        keep[kk, th, 0, :, inner, :] = part[1]
                        send1[kk, th, 2, :, rows, :] = part[3].astype(BF16)
                    else:
                        send1[kk, th, 0, :, rows, :] = part[1].astype(BF16)
                        keep[kk, th, 1, :, inner, :] = part[3]
            return carry

        lax.fori_loop(0, 4, body, 0)

    def copy1(kk, th, kind, direction, spot):
        slot = 1 if kind == 0 else (0 if direction == 0 else 2)
        half = direction if kind in (0, 2) else 1 - direction
        return pltpu.make_async_remote_copy(
            src_ref=send1.at[kk, th, slot, spot, half_rows(half)],
            dst_ref=recv1.at[kk, th, kind, direction, spot],
            send_sem=s1_sem.at[kk, th, kind, direction, spot],
            recv_sem=r1_sem.at[kk, th, kind, direction, spot],
            device_id=neighbour(kk, 1, direction),
            device_id_type=MESH,
        )

    def copy2(kk, th, kind, direction):
        slot = 1 if kind == 0 else (0 if direction == 0 else 2)
        half = direction if kind in (0, 2) else 1 - direction
        return pltpu.make_async_remote_copy(
            src_ref=send2.at[kk, th, slot, half_rows(half)],
            dst_ref=recv2.at[kk, th, kind, direction],
            send_sem=s2_sem.at[kk, th, kind, direction],
            recv_sem=r2_sem.at[kk, th, kind, direction],
            device_id=neighbour(kk, 2, direction),
            device_id_type=MESH,
        )

    def copy3(kk, th, off):
        block = (rcv + off) % BLOCKS
        return pltpu.make_async_remote_copy(
            src_ref=send3.at[kk, th, pl.ds(pl.multiple_of(block * CAP, CAP), CAP)],
            dst_ref=recv3.at[kk, th, pl.ds(pl.multiple_of(rcv * CAP, CAP), CAP)],
            send_sem=s3_sem.at[kk, th, off - 1],
            recv_sem=r3_sem.at[kk, th, off - 1],
            device_id=(shot, block),
            device_id_type=MESH,
        )

    pairs = [(kk, direction) for kk in range(2) for direction in range(2)]

    def start1(th, kind, spots, directions=(0, 1)):
        for spot in spots:
            for kk in range(2):
                for direction in directions:
                    copy1(kk, th, kind, direction, spot).start()

    def accumulate1(th, spot):
        for kk, direction in pairs:
            copy1(kk, th, 0, direction, spot).wait_recv()
            total = keep[kk, th, direction, spot] + recv1[kk, th, 0, direction, spot].astype(F32)
            send1[kk, th, 0 if direction == 0 else 2, spot, half_rows(direction), :] = total.astype(BF16)
            copy1(kk, th, 2, direction, spot).start()

    def finish1(kk, th, spot):
        for direction in range(2):
            copy1(kk, th, 1, direction, spot).wait_recv()
        for direction in range(2):
            copy1(kk, th, 2, direction, spot).wait_recv()
        sums = []
        for half in range(2):
            sums.append(
                own[kk, th, spot, half_rows(half), :]
                + recv1[kk, th, 2, half, spot].astype(F32)
                + recv1[kk, th, 1, 1 - half, spot].astype(F32)
            )
        return sums

    def stage2_start(th):
        for kk in range(2):
            low, high = finish1(kk, th, 0)
            send2[kk, th, 1, half_rows(0), :] = low.astype(BF16)
            send2[kk, th, 1, half_rows(1), :] = high.astype(BF16)
            copy2(kk, th, 0, 0).start()
            copy2(kk, th, 0, 1).start()
        for kk in range(2):
            low, high = finish1(kk, th, 1)
            own[kk, th, 1, half_rows(0), :] = low
            send2[kk, th, 0, half_rows(1), :] = high.astype(BF16)
            copy2(kk, th, 1, 0).start()
            low, high = finish1(kk, th, 2)
            send2[kk, th, 2, half_rows(0), :] = low.astype(BF16)
            own[kk, th, 2, half_rows(1), :] = high
            copy2(kk, th, 1, 1).start()

    def accumulate2(th):
        for kk, direction in pairs:
            copy2(kk, th, 0, direction).wait_recv()
            spot = 1 + direction
            total = own[kk, th, spot, half_rows(direction), :] + recv2[kk, th, 0, direction].astype(F32)
            send2[kk, th, 0 if direction == 0 else 2, half_rows(direction), :] = total.astype(BF16)
            copy2(kk, th, 2, direction).start()

    def exchange(th):
        for kk in range(2):
            sums = finish1(kk, th, 3)
            for kind in (1, 2):
                for direction in range(2):
                    copy2(kk, th, kind, direction).wait_recv()
            for half in range(2):
                total = sums[half] + recv2[kk, th, 2, half].astype(F32) + recv2[kk, th, 1, 1 - half].astype(F32)
                seen = obsbuf[kk, half_rows(half), th * LANES:(th + 1) * LANES].astype(F32)
                sums[half] = (total - seen).astype(BF16)
            residual = jnp.concatenate(sums, axis=0)
            packed = jnp.dot(sel[...], residual, preferred_element_type=F32).astype(BF16)
            send3[kk, th] = packed
            for off in (4, 3, 5, 2, 6, 1, 7):
                copy3(kk, th, off).start()
            here = pl.ds(pl.multiple_of(rcv * CAP, CAP), CAP)
            recv3[kk, th, here, :] = send3[kk, th, here, :]

    def inject(th):
        for kk in range(2):
            for off in range(1, BLOCKS):
                copy3(kk, th, off).wait_recv()
            obuf[kk, :, th * LANES:(th + 1) * LANES] = jnp.dot(
                injc[...], recv3[kk, th], preferred_element_type=F32
            )

    loads[1].wait()
    encode(0, 0)
    loads[2].wait()
    encode(0, 1)
    pl.semaphore_wait(barrier, 4 + BLOCKS - 1)
    start1(0, 0, (0, 1, 2, 3), (0,))
    start1(0, 1, (0, 1), (1,))
    loads[3].wait()
    encode(1, 2)
    loads[4].wait()
    encode(1, 3)
    start1(0, 0, (0, 1, 2, 3), (1,))
    start1(0, 1, (0, 1, 2), (0,))
    start1(0, 1, (2,), (1,))

    for load in loads[5:]:
        load.wait()
    before = (iota((RCV, RCV), 0) < iota((RCV, RCV), 1)).astype(BF16)

    def rank_of(window):
        named = (iota((BLOCKS, RCV), 0) == window).astype(F32)
        count = jnp.dot(named.astype(BF16), before, preferred_element_type=F32)
        return jnp.sum(named * count, axis=0, keepdims=True).astype(I32)

    mine = blk[:, pl.ds(pl.multiple_of(rcv * RCV, RCV), RCV)]
    sel[...] = (iota((BLOCKS * CAP, RCV), 0) == mine * CAP + rank_of(mine)).astype(BF16)
    for pair in range(BLOCKS // 2):
        chosen = []
        for side in range(2):
            start = (2 * pair + side) * RCV
            window = blk[:, start:start + RCV]
            slot = jnp.where(window == rcv, side * CAP + rank_of(window), -1)
            chosen.append((iota((2 * CAP, RCV), 0) == slot).astype(BF16))
            spread = jnp.zeros((GRID, RCV), F32)
            for which in range(STENCIL):
                point = idx[which:which + 1, start:start + RCV]
                weight = wgt[which:which + 1, start:start + RCV]
                spread = spread + jnp.where(iota((GRID, RCV), 0) == point, weight, 0.0)
            inj[:, side * RCV:(side + 1) * RCV] = spread.astype(BF16)
        injc[:, pair * LANES:(pair + 1) * LANES] = lax.dot_general(
            inj[...], jnp.concatenate(chosen, axis=1), (((1,), (1,)), ((), ())), preferred_element_type=F32
        ).astype(BF16)

    for spot in (0, 1, 2):
        accumulate1(0, spot)
    start1(1, 0, (0, 1, 2, 3))
    stage2_start(0)
    start1(1, 1, (0, 1, 2))
    accumulate2(0)
    for spot in (0, 1, 2):
        accumulate1(1, spot)
    start1(0, 1, (3,))
    accumulate1(0, 3)
    stage2_start(1)
    start1(1, 1, (3,))
    accumulate1(1, 3)
    exchange(0)
    accumulate2(1)
    exchange(1)
    inject(0)
    inject(1)
    put = pltpu.make_async_copy(obuf, out_hbm, out_sem)
    put.start()
    for kk, direction in pairs:
        for th in range(2):
            for kind in range(3):
                for spot in range(4):
                    copy1(kk, th, kind, direction, spot).wait_send()
                copy2(kk, th, kind, direction).wait_send()
    for kk in range(2):
        for th in range(2):
            for off in range(1, BLOCKS):
                copy3(kk, th, off).wait_send()
    put.wait()


def local(shot_data, code, observed, block_of, stencil_index, stencil_weight):
    dma = pltpu.SemaphoreType.DMA
    any_space = pl.BlockSpec(memory_space=pl.ANY)
    return pl.pallas_call(
        kernel,
        out_shape=jax.ShapeDtypeStruct((2, GRID, SAMPLES), F32),
        in_specs=[any_space] * 6,
        out_specs=any_space,
        scratch_shapes=[
            pltpu.VMEM((SHOTS_DEV, RCV, SAMPLES), BF16),
            pltpu.VMEM((SUPERS, SHOTS_DEV), I32),
            pltpu.VMEM((2, RCV, SAMPLES), BF16),
            pltpu.VMEM((1, BLOCKS * RCV), I32),
            pltpu.VMEM((STENCIL, BLOCKS * RCV), I32),
            pltpu.VMEM((STENCIL, BLOCKS * RCV), F32),
            pltpu.VMEM((ROWS, DEPTH), BF16),
            pltpu.VMEM((GRID, 2 * RCV), BF16),
            pltpu.VMEM((GRID, BLOCKS * CAP), BF16),
            pltpu.VMEM((BLOCKS * CAP, RCV), BF16),
            pltpu.VMEM((2, GRID, SAMPLES), F32),
            pltpu.VMEM((2, 2, 4, RCV, LANES), F32),
            pltpu.VMEM((2, 2, 2, 4, HALF, LANES), F32),
            pltpu.VMEM((2, 2, 3, 4, RCV, LANES), BF16),
            pltpu.VMEM((2, 2, 3, 2, 4, HALF, LANES), BF16),
            pltpu.VMEM((2, 2, 3, RCV, LANES), BF16),
            pltpu.VMEM((2, 2, 3, 2, HALF, LANES), BF16),
            pltpu.VMEM((2, 2, BLOCKS * CAP, LANES), BF16),
            pltpu.VMEM((2, 2, BLOCKS * CAP, LANES), BF16),
            dma((9,)),
            dma,
            dma((2, 2, 3, 2, 4)),
            dma((2, 2, 3, 2, 4)),
            dma((2, 2, 3, 2)),
            dma((2, 2, 3, 2)),
            dma((2, 2, BLOCKS - 1)),
            dma((2, 2, BLOCKS - 1)),
        ],
        compiler_params=pltpu.CompilerParams(
            collective_id=0, has_side_effects=True, vmem_limit_bytes=60 * 1024 * 1024
        ),
    )(shot_data, code, observed, block_of.T, stencil_index.T, stencil_weight.T)


def solution(mesh):
    split = P("shot", "rcv", None)
    return jax.shard_map(
        local,
        mesh=mesh,
        in_specs=(split, P(None, "shot"), split, P(), P(), P()),
        out_specs=split,
        check_vma=False,
    )
```

time: 153 us -> 45 us (0.29)
  waiting for transfers between devices: 113 us -> 0 us
  Pallas kernels: 0 us -> 43 us
  between operations: 13.5 us -> 0.01 us
  matrix products: 10.9 us -> 0 us
  local copies, waits for them, and re-layouts: 12.6 us -> 1.87 us
  other arithmetic: 2.51 us -> 0 us
    unnamed x3 -> x0, waiting for transfers between devices: 86.8 us -> none
    pallas_call x0 -> x1, Pallas kernels: none -> 43 us  [local(): pl.pallas_call(kernel, out_shape=jax.ShapeDtypeStruct((2, GRID, SAMPLES),...]
    convert_element_type x1 -> x0, waiting for transfers between devices: 26.5 us -> none  [reference(): residual = (supershot - observed.astype(jnp.float32)).astype(jnp.bfloat16)]
    dot_general x2 -> x0, matrix products: 10.9 us -> none  [the longest x1 8.03 us: reference(): jnp.dot(code.astype(jnp.bfloat16), flat_rows, preferred_element_type=jnp....]
    dot_general x1 -> x0, local copies, waits for them, and re-layouts: 9.94 us -> none  [reference(): jnp.dot(code.astype(jnp.bfloat16), flat_rows, preferred_element_type=jnp....]
    convert_element_type x1 -> x0, other arithmetic: 1.8 us -> none  [reference(): residual = (supershot - observed.astype(jnp.float32)).astype(jnp.bfloat16)]
  transfers between devices with their start and end apart: 2 -> 0, of which waited for: 2 -> 0; matrix products, arithmetic and copies ran while one was open for 1% -> 0% of each run, Pallas kernels for 0% -> 0%
where the time goes in v1:
time: 45 us; the launch traced here: 44.9 us
  Pallas kernels  43 us (96%)
  local copies, waits for them, and re-layouts  1.87 us (4%)
    pallas_call x1, Pallas kernels, local(): pl.pallas_call(kernel, out_shape=jax.ShapeDtypeStruct((2, GRID, SAMPLES),...  43 us
    unnamed x1, local copies, waits for them, and re-layouts  1.87 us

profile of v1, /device:TPU:1, one launch (start us, length us, event | category | flops | bytes accessed | tf_op | source)
XLA Modules:
  0.0 44.9 jit_solution(1468725988672828461)
XLA Ops:
  0.0 43.0 %shard_map.64 = f32[2,256,256]{2,1,0:T(8,128)} custom-call(bf16[32,256,256]{2,1,0:T(8,128)(2,1)} %shot_hbm.1, s32[32,32]{1,0:T(8,128)} %code_hbm.1, bf16[2,256,256]{2,1,0:T(8,128)(2,1)} %obs_hbm.1, s32[1,2048]{1,0:T(1,128)} %bitcast.5, s32[4,2048]{1,0:T(4,128)} %bitcast.3, f32[4,2048]{1,0:T(4,128)} %bitcast.4), custom_call_target="tpu_custom_call" | custom-call | tf_op jit(solution)/shard_map/pallas_call | solution.py:304
  43.0 1.9 %copy.8 = f32[2,256,256]{2,1,0:T(8,128)} copy(f32[2,256,256]{2,1,0:T(8,128)} %shard_map.64) | data formatting | bytes 1048576

commit v2 on v1

v2 whole, which is shorter than its diff:
```python
import jax
import jax.numpy as jnp
from jax import lax
from jax.experimental import pallas as pl
from jax.experimental.pallas import tpu as pltpu
from jax.sharding import PartitionSpec as P

SUPERS = 32
GRID = 256
STENCIL = 4
BLOCKS = 8
CAP = 64
RING = 4
RCV = 256
HALF = RCV // 2
SAMPLES = 256
LANES = 128
SHOTS_DEV = 32
GROUP = 16
ROWS = SUPERS * GROUP
DEPTH = SHOTS_DEV * GROUP
ORDER = (2, 1, 3, 0)
F32, BF16, I32 = jnp.float32, jnp.bfloat16, jnp.int32
MESH = pl.DeviceIdType.MESH
SCHEDULE = (
    ("plain", 1, 0, 1), ("relay", 0, 1, 0), ("relay", 1, 1, 0), ("relay", 1, 1, 2),
    ("plain", 0, 0, 1), ("relay", 0, 1, 1), ("relay", 0, 1, 2), ("plain", 1, 0, 0),
    ("plain", 1, 0, 2), ("add", 0, 0, 0), ("add", 1, 0, 0), ("relay", 1, 1, 1),
    ("plain", 0, 0, 0), ("plain", 0, 1, 0), ("add", 0, 0, 1), ("add", 1, 0, 1),
    ("plain", 1, 1, 1), ("plain", 0, 0, 2), ("add", 0, 1, 0), ("plain", 1, 1, 0),
    ("add", 1, 0, 2), ("add", 1, 1, 0), ("plain", 0, 1, 1), ("add", 0, 0, 2),
    ("plain", 0, 1, 2), ("turn", 1, 0, 0), ("turn", 0, 0, 0), ("add", 1, 1, 1),
    ("add", 0, 1, 1), ("relay", 1, 1, 3), ("plain", 1, 1, 2), ("add", 0, 1, 2),
    ("turn", 0, 1, 0), ("add", 1, 1, 2), ("relay", 0, 1, 3), ("add", 0, 0, 3),
    ("turn", 0, 0, 2), ("turn", 1, 1, 0), ("plain", 0, 0, 3), ("turn", 1, 0, 2),
    ("turn", 0, 0, 1), ("add2", 0, 0), ("turn", 1, 0, 1), ("add2", 1, 0),
    ("add", 1, 0, 3), ("plain", 1, 0, 3), ("turn", 0, 1, 1), ("plain", 0, 1, 3),
    ("turn", 0, 1, 2), ("add", 0, 1, 3), ("turn", 1, 1, 1), ("add2", 0, 1),
    ("turn", 1, 1, 2), ("plain", 1, 1, 3), ("add2", 1, 1), ("add", 1, 1, 3),
    ("swap", 0, 0), ("swap", 1, 0), ("swap", 0, 1), ("swap", 1, 1),
)


def iota(shape, dim):
    return lax.broadcasted_iota(I32, shape, dim)


def encoding_rows(shape, y, z):
    row = iota(shape, 0)
    kk = row // (ROWS // 2)
    first = (row // (4 * GROUP)) % 4
    spot = (row // GROUP) % 4
    second = jnp.where(spot == 0, 2, jnp.where(spot == 1, 1, jnp.where(spot == 2, 3, 0)))
    dy = jnp.where(kk == 0, first, second)
    dz = jnp.where(kk == 0, second, first)
    return 8 * ((y + dy) % 4) + 2 * ((z + dz) % 4) + kk


def kernel(
    shot_hbm, code_hbm, obs_hbm, blk_hbm, idx_hbm, wgt_hbm, out,
    xbuf, codebuf, obsbuf, blk, idx, wgt, enc, inj, injc, sel,
    own, keep, send1, send2, send3, got_relay, got_turn, got_last, got_relay2, got_swap,
    load_sem, s_relay, s_turn, s_last, s_relay2, s_swap, r_relay, r_turn, r_last, r_relay2, r_swap,
):
    shot, rcv = lax.axis_index("shot"), lax.axis_index("rcv")
    y, z = shot // 4, shot % 4

    def at_shot(dy, dz):
        return (((y + dy) % 4) * 4 + (z + dz) % 4, rcv)

    def neighbour(kk, stage, direction):
        step = 1 if direction == 0 else 3
        along_y = (kk == 0) == (stage == 1)
        return at_shot(step, 0) if along_y else at_shot(0, step)

    loads = [pltpu.make_async_copy(code_hbm, codebuf, load_sem.at[0])]
    for chunk in range(4):
        rows = pl.ds(chunk * 64, 64)
        loads.append(pltpu.make_async_copy(shot_hbm.at[:, rows], xbuf.at[:, rows], load_sem.at[1 + chunk]))
    loads.append(pltpu.make_async_copy(obs_hbm, obsbuf, load_sem.at[5]))
    loads.append(pltpu.make_async_copy(blk_hbm, blk, load_sem.at[6]))
    loads.append(pltpu.make_async_copy(idx_hbm, idx, load_sem.at[7]))
    loads.append(pltpu.make_async_copy(wgt_hbm, wgt, load_sem.at[8]))
    for load in loads:
        load.start()

    barrier = pltpu.get_barrier_semaphore()
    for peer in (at_shot(1, 0), at_shot(3, 0), at_shot(0, 1), at_shot(0, 3)):
        pl.semaphore_signal(barrier, inc=1, device_id=peer, device_id_type=MESH)
    for off in range(1, BLOCKS):
        pl.semaphore_signal(barrier, inc=1, device_id=(shot, (rcv + off) % BLOCKS), device_id_type=MESH)

    loads[0].wait()
    pick = (encoding_rows((ROWS, SUPERS), y, z) == iota((ROWS, SUPERS), 1)).astype(BF16)
    codes = jnp.dot(pick, codebuf[...].astype(F32).astype(BF16), preferred_element_type=F32).astype(BF16)
    widen = (iota((SHOTS_DEV, DEPTH), 1) // GROUP == iota((SHOTS_DEV, DEPTH), 0)).astype(BF16)
    wide = jnp.dot(codes, widen, preferred_element_type=F32)
    same = iota((ROWS, DEPTH), 0) % GROUP == iota((ROWS, DEPTH), 1) % GROUP
    enc[...] = jnp.where(same, wide, 0.0).astype(BF16)

    def half_rows(half):
        return pl.ds(half * HALF, HALF)

    def encode(half, chunk):
        def body(step, carry):
            r0 = pl.multiple_of(chunk * 64 + step * GROUP, GROUP)
            data = xbuf[:, pl.ds(r0, GROUP), :].reshape(DEPTH, SAMPLES)
            for kk in range(2):
                product = jnp.dot(enc[kk * 256:(kk + 1) * 256, :], data, preferred_element_type=F32)
                product = product.reshape(4, 4, GROUP, SAMPLES)
                for th in range(2):
                    part = product[:, :, :, th * LANES:(th + 1) * LANES]
                    rows = pl.ds(r0, GROUP)
                    inner = pl.ds(pl.multiple_of(r0 - half * HALF, GROUP), GROUP)
                    own[kk, th, :, rows, :] = part[0]
                    send1[kk, th, 1, :, rows, :] = part[2].astype(BF16)
                    if half == 0:
                        keep[kk, th, 0, :, inner, :] = part[1]
                        send1[kk, th, 2, :, rows, :] = part[3].astype(BF16)
                    else:
                        send1[kk, th, 0, :, rows, :] = part[1].astype(BF16)
                        keep[kk, th, 1, :, inner, :] = part[3]
            return carry

        lax.fori_loop(0, 4, body, 0, unroll=True)

    def copy1(kk, th, kind, direction, spot):
        unit = 2 * kk + th
        slot = 1 if kind == 0 else (0 if direction == 0 else 2)
        half = direction if kind in (0, 2) else 1 - direction
        if kind == 0:
            place, sems = got_relay.at[unit * 4 + spot, direction], (s_relay, r_relay.at[unit * 4 + spot])
        elif spot < 3:
            place, sems = got_turn.at[unit * 3 + spot, 2 * (kind - 1) + direction], (s_turn, r_turn.at[unit * 3 + spot])
        else:
            place, sems = got_last.at[unit, 2 * (kind - 1) + direction], (s_last, r_last.at[unit])
        return pltpu.make_async_remote_copy(
            src_ref=send1.at[kk, th, slot, spot, half_rows(half)],
            dst_ref=place,
            send_sem=sems[0],
            recv_sem=sems[1],
            device_id=neighbour(kk, 1, direction),
            device_id_type=MESH,
        )

    def copy2(kk, th, kind, direction):
        unit = 2 * kk + th
        slot = 1 if kind == 0 else (0 if direction == 0 else 2)
        half = direction if kind in (0, 2) else 1 - direction
        if kind == 0:
            place, sems = got_relay2.at[unit, direction], (s_relay2, r_relay2.at[unit])
        else:
            place, sems = got_last.at[unit, 2 + 2 * kind + direction], (s_last, r_last.at[unit])
        return pltpu.make_async_remote_copy(
            src_ref=send2.at[kk, th, slot, half_rows(half)],
            dst_ref=place,
            send_sem=sems[0],
            recv_sem=sems[1],
            device_id=neighbour(kk, 2, direction),
            device_id_type=MESH,
        )

    def copy3(kk, th, off):
        block = (rcv + off) % BLOCKS
        return pltpu.make_async_remote_copy(
            src_ref=send3.at[kk, th, pl.ds(pl.multiple_of(block * CAP, CAP), CAP)],
            dst_ref=got_swap.at[2 * kk + th, pl.ds(pl.multiple_of(rcv * CAP, CAP), CAP)],
            send_sem=s_swap,
            recv_sem=r_swap.at[2 * kk + th],
            device_id=(shot, block),
            device_id_type=MESH,
        )

    def arrived(place, sem):
        pltpu.make_async_copy(place, place, sem).wait()

    def relay(kk, th, spot, directions=(0, 1)):
        for direction in directions:
            copy1(kk, th, 0, direction, spot).start()

    def plain(kk, th, spot, directions=(0, 1)):
        for direction in directions:
            copy1(kk, th, 1, direction, spot).start()

    def add(kk, th, spot):
        at = (2 * kk + th) * 4 + spot
        arrived(got_relay.at[at], r_relay.at[at])
        for direction in range(2):
            total = keep[kk, th, direction, spot] + got_relay[at, direction].astype(F32)
            send1[kk, th, 0 if direction == 0 else 2, spot, half_rows(direction), :] = total.astype(BF16)
            copy1(kk, th, 2, direction, spot).start()

    def summed(kk, th, spot, plain_at, added_at):
        return [
            own[kk, th, spot, half_rows(half), :] + added_at[half].astype(F32) + plain_at[1 - half].astype(F32)
            for half in range(2)
        ]

    def turn(kk, th, spot):
        at = (2 * kk + th) * 3 + spot
        arrived(got_turn.at[at], r_turn.at[at])
        low, high = summed(
            kk, th, spot, [got_turn[at, 0], got_turn[at, 1]], [got_turn[at, 2], got_turn[at, 3]]
        )
        if spot == 0:
            send2[kk, th, 1, half_rows(0), :] = low.astype(BF16)
            send2[kk, th, 1, half_rows(1), :] = high.astype(BF16)
            copy2(kk, th, 0, 0).start()
            copy2(kk, th, 0, 1).start()
        elif spot == 1:
            own[kk, th, 1, half_rows(0), :] = low
            send2[kk, th, 0, half_rows(1), :] = high.astype(BF16)
            copy2(kk, th, 1, 0).start()
        else:
            send2[kk, th, 2, half_rows(0), :] = low.astype(BF16)
            own[kk, th, 2, half_rows(1), :] = high
            copy2(kk, th, 1, 1).start()

    def add2(kk, th):
        unit = 2 * kk + th
        arrived(got_relay2.at[unit], r_relay2.at[unit])
        for direction in range(2):
            total = own[kk, th, 1 + direction, half_rows(direction), :] + got_relay2[unit, direction].astype(F32)
            send2[kk, th, 0 if direction == 0 else 2, half_rows(direction), :] = total.astype(BF16)
            copy2(kk, th, 2, direction).start()

    def swap(kk, th):
        unit = 2 * kk + th
        arrived(got_last.at[unit], r_last.at[unit])
        last = [got_last[unit, part] for part in range(8)]
        sums = summed(kk, th, 3, last[0:2], last[2:4])
        for half in range(2):
            total = sums[half] + last[6 + half].astype(F32) + last[5 - half].astype(F32)
            seen = obsbuf[kk, half_rows(half), th * LANES:(th + 1) * LANES].astype(F32)
            sums[half] = (total - seen).astype(BF16)
        residual = jnp.concatenate(sums, axis=0)
        packed = jnp.dot(sel[...], residual, preferred_element_type=F32).astype(BF16)
        send3[kk, th] = packed
        for off in (4, 3, 5, 2, 6, 1, 7):
            copy3(kk, th, off).start()
        here = pl.ds(pl.multiple_of(rcv * CAP, CAP), CAP)
        got_swap[unit, here, :] = send3[kk, th, here, :]

    def inject(kk, th):
        unit = 2 * kk + th
        arrived(got_swap.at[unit, pl.ds(0, (BLOCKS - 1) * CAP)], r_swap.at[unit])
        out[kk, :, th * LANES:(th + 1) * LANES] = jnp.dot(
            injc[...], got_swap[unit], preferred_element_type=F32
        )

    def tables():
        for load in loads[5:]:
            load.wait()
        before = (iota((RCV, RCV), 0) < iota((RCV, RCV), 1)).astype(BF16)

        def rank_of(window):
            named = (iota((BLOCKS, RCV), 0) == window).astype(F32)
            count = jnp.dot(named.astype(BF16), before, preferred_element_type=F32)
            return jnp.sum(named * count, axis=0, keepdims=True).astype(I32)

        mine = blk[:, pl.ds(pl.multiple_of(rcv * RCV, RCV), RCV)]
        sel[...] = (iota((BLOCKS * CAP, RCV), 0) == mine * CAP + rank_of(mine)).astype(BF16)
        for pair in range(BLOCKS // 2):
            chosen = []
            for side in range(2):
                start = (2 * pair + side) * RCV
                window = blk[:, start:start + RCV]
                slot = jnp.where(window == rcv, side * CAP + rank_of(window), -1)
                chosen.append((iota((2 * CAP, RCV), 0) == slot).astype(BF16))
                spread = jnp.zeros((GRID, RCV), F32)
                for which in range(STENCIL):
                    point = idx[which:which + 1, start:start + RCV]
                    weight = wgt[which:which + 1, start:start + RCV]
                    spread = spread + jnp.where(iota((GRID, RCV), 0) == point, weight, 0.0)
                inj[:, side * RCV:(side + 1) * RCV] = spread.astype(BF16)
            injc[:, pair * LANES:(pair + 1) * LANES] = lax.dot_general(
                inj[...], jnp.concatenate(chosen, axis=1), (((1,), (1,)), ((), ())), preferred_element_type=F32
            ).astype(BF16)

    loads[1].wait()
    encode(0, 0)
    loads[2].wait()
    encode(0, 1)
    pl.semaphore_wait(barrier, 4 + BLOCKS - 1)
    for spot in range(4):
        for kk in range(2):
            relay(kk, 0, spot, (0,))
    for spot in range(2):
        for kk in range(2):
            plain(kk, 0, spot, (1,))
    loads[3].wait()
    encode(1, 2)
    loads[4].wait()
    encode(1, 3)
    for spot in range(4):
        for kk in range(2):
            relay(kk, 0, spot, (1,))

    steps = {"relay": relay, "plain": plain, "add": add, "turn": turn, "add2": add2, "swap": swap}
    waiting = False
    for name, kk, th, *spot in SCHEDULE:
        if name not in ("relay", "plain") and not waiting:
            tables()
            waiting = True
        if name == "plain" and th == 0 and spot[0] < 2:
            plain(kk, 0, spot[0], (0,))
        else:
            steps[name](kk, th, *spot)
    for name, kk, th in SCHEDULE[-4:]:
        inject(kk, th)
    arrived(got_relay, s_relay)
    arrived(got_turn, s_turn)
    arrived(got_last, s_last)
    arrived(got_relay2, s_relay2)
    arrived(got_relay.at[pl.ds(0, BLOCKS - 1)], s_swap)


def local(shot_data, code, observed, block_of, stencil_index, stencil_weight):
    dma = pltpu.SemaphoreType.DMA
    any_space = pl.BlockSpec(memory_space=pltpu.HBM)
    return pl.pallas_call(
        kernel,
        out_shape=jax.ShapeDtypeStruct((2, GRID, SAMPLES), F32),
        in_specs=[any_space] * 6,
        out_specs=pl.BlockSpec(memory_space=pltpu.VMEM),
        scratch_shapes=[
            pltpu.VMEM((SHOTS_DEV, RCV, SAMPLES), BF16),
            pltpu.VMEM((SUPERS, SHOTS_DEV), I32),
            pltpu.VMEM((2, RCV, SAMPLES), BF16),
            pltpu.VMEM((1, BLOCKS * RCV), I32),
            pltpu.VMEM((STENCIL, BLOCKS * RCV), I32),
            pltpu.VMEM((STENCIL, BLOCKS * RCV), F32),
            pltpu.VMEM((ROWS, DEPTH), BF16),
            pltpu.VMEM((GRID, 2 * RCV), BF16),
            pltpu.VMEM((GRID, BLOCKS * CAP), BF16),
            pltpu.VMEM((BLOCKS * CAP, RCV), BF16),
            pltpu.VMEM((2, 2, 4, RCV, LANES), F32),
            pltpu.VMEM((2, 2, 2, 4, HALF, LANES), F32),
            pltpu.VMEM((2, 2, 3, 4, RCV, LANES), BF16),
            pltpu.VMEM((2, 2, 3, RCV, LANES), BF16),
            pltpu.VMEM((2, 2, BLOCKS * CAP, LANES), BF16),
            pltpu.VMEM((16, 2, HALF, LANES), BF16),
            pltpu.VMEM((12, 4, HALF, LANES), BF16),
            pltpu.VMEM((4, 8, HALF, LANES), BF16),
            pltpu.VMEM((4, 2, HALF, LANES), BF16),
            pltpu.VMEM((4, BLOCKS * CAP, LANES), BF16),
            dma((9,)),
            dma,
            dma,
            dma,
            dma,
            dma,
            dma((16,)),
            dma((12,)),
            dma((4,)),
            dma((4,)),
            dma((4,)),
        ],
        compiler_params=pltpu.CompilerParams(
            collective_id=0, has_side_effects=True, vmem_limit_bytes=52 * 1024 * 1024
        ),
    )(*[pltpu.with_memory_space_constraint(v, pltpu.HBM) for v in (shot_data, code, observed, block_of.T, stencil_index.T, stencil_weight.T)])


def solution(mesh):
    split = P("shot", "rcv", None)
    return jax.shard_map(
        local,
        mesh=mesh,
        in_specs=(split, P(None, "shot"), split, P(), P(), P()),
        out_specs=split,
        check_vma=False,
    )
```

time: 45 us -> 37.2 us (0.83)
  Pallas kernels: 43 us -> 36.2 us
  local copies, waits for them, and re-layouts: 1.87 us -> 0.8 us
    pallas_call x1, Pallas kernels: 43 us -> 36.2 us  [local(): pl.pallas_call(kernel, out_shape=jax.ShapeDtypeStruct((2, GRID, SAMPLES),...]
    unnamed x1, local copies, waits for them, and re-layouts: 1.87 us -> 0.8 us
where the time goes in v2:
time: 37.2 us; the launch traced here: 37 us
  Pallas kernels  36.2 us (97%)
  local copies, waits for them, and re-layouts  0.8 us (2%)
    pallas_call x1, Pallas kernels, local(): pl.pallas_call(kernel, out_shape=jax.ShapeDtypeStruct((2, GRID, SAMPLES),...  36.2 us
    unnamed x1, local copies, waits for them, and re-layouts  0.8 us

profile of v2, /device:TPU:1, one launch (start us, length us, event | category | flops | bytes accessed | tf_op | source)
XLA Modules:
  0.0 37.0 jit_solution(7324499010308884994)
XLA Ops:
  0.0 36.2 %shard_map.64 = f32[2,256,256]{2,1,0:T(8,128)S(1)} custom-call(bf16[32,256,256]{2,1,0:T(8,128)(2,1)} %shot_hbm.1, s32[32,32]{1,0:T(8,128)} %code_hbm.1, bf16[2,256,256]{2,1,0:T(8,128)(2,1)} %obs_hbm.1, s32[1,2048]{1,0:T(1,128)} %bitcast.5, s32[4,2048]{1,0:T(4,128)} %bitcast.3, f32[4,2048]{1,0:T(4,128)} %bitcast.4), custom_call_target="tpu_custom_call" | custom-call | tf_op jit(solution)/shard_map/pallas_call | solution.py:321
  36.2 0.8 %copy.8 = f32[2,256,256]{2,1,0:T(8,128)} copy(f32[2,256,256]{2,1,0:T(8,128)S(1)} %shard_map.64) | data formatting | bytes 1048576

commit v3 on v2

--- a/solution.py
+++ b/solution.py
@@ -23,20 +23,20 @@
 F32, BF16, I32 = jnp.float32, jnp.bfloat16, jnp.int32
 MESH = pl.DeviceIdType.MESH
 SCHEDULE = (
-    ("plain", 1, 0, 1), ("relay", 0, 1, 0), ("relay", 1, 1, 0), ("relay", 1, 1, 2),
-    ("plain", 0, 0, 1), ("relay", 0, 1, 1), ("relay", 0, 1, 2), ("plain", 1, 0, 0),
-    ("plain", 1, 0, 2), ("add", 0, 0, 0), ("add", 1, 0, 0), ("relay", 1, 1, 1),
-    ("plain", 0, 0, 0), ("plain", 0, 1, 0), ("add", 0, 0, 1), ("add", 1, 0, 1),
-    ("plain", 1, 1, 1), ("plain", 0, 0, 2), ("add", 0, 1, 0), ("plain", 1, 1, 0),
-    ("add", 1, 0, 2), ("add", 1, 1, 0), ("plain", 0, 1, 1), ("add", 0, 0, 2),
-    ("plain", 0, 1, 2), ("turn", 1, 0, 0), ("turn", 0, 0, 0), ("add", 1, 1, 1),
-    ("add", 0, 1, 1), ("relay", 1, 1, 3), ("plain", 1, 1, 2), ("add", 0, 1, 2),
-    ("turn", 0, 1, 0), ("add", 1, 1, 2), ("relay", 0, 1, 3), ("add", 0, 0, 3),
-    ("turn", 0, 0, 2), ("turn", 1, 1, 0), ("plain", 0, 0, 3), ("turn", 1, 0, 2),
-    ("turn", 0, 0, 1), ("add2", 0, 0), ("turn", 1, 0, 1), ("add2", 1, 0),
-    ("add", 1, 0, 3), ("plain", 1, 0, 3), ("turn", 0, 1, 1), ("plain", 0, 1, 3),
-    ("turn", 0, 1, 2), ("add", 0, 1, 3), ("turn", 1, 1, 1), ("add2", 0, 1),
-    ("turn", 1, 1, 2), ("plain", 1, 1, 3), ("add2", 1, 1), ("add", 1, 1, 3),
+    ("relay", 1, 1, 0), ("plain", 0, 0, 0), ("relay", 0, 1, 0), ("plain", 0, 0, 1),
+    ("plain", 1, 0, 0), ("plain", 1, 0, 1), ("plain", 1, 0, 2), ("relay", 0, 1, 2),
+    ("plain", 1, 1, 0), ("relay", 1, 1, 3), ("plain", 0, 1, 0), ("plain", 0, 0, 2),
+    ("add", 0, 0, 0), ("relay", 0, 1, 1), ("relay", 1, 1, 1), ("add", 1, 0, 0),
+    ("relay", 1, 1, 2), ("add", 0, 0, 1), ("plain", 1, 1, 1), ("add", 1, 0, 2),
+    ("add", 0, 0, 2), ("add", 1, 1, 0), ("add", 0, 1, 0), ("add", 0, 1, 2),
+    ("relay", 0, 1, 3), ("add", 1, 0, 1), ("turn", 0, 0, 0), ("plain", 0, 1, 1),
+    ("plain", 1, 1, 2), ("add", 0, 1, 1), ("turn", 1, 0, 0), ("add", 1, 1, 2),
+    ("add", 1, 1, 1), ("plain", 0, 1, 2), ("turn", 0, 1, 0), ("turn", 0, 0, 2),
+    ("plain", 0, 0, 3), ("turn", 1, 1, 0), ("add", 0, 0, 3), ("turn", 0, 0, 1),
+    ("turn", 1, 0, 1), ("add2", 0, 0), ("plain", 1, 0, 3), ("turn", 1, 0, 2),
+    ("add", 1, 0, 3), ("add2", 1, 0), ("add", 0, 1, 3), ("plain", 0, 1, 3),
+    ("turn", 0, 1, 1), ("turn", 1, 1, 2), ("turn", 0, 1, 2), ("add2", 0, 1),
+    ("plain", 1, 1, 3), ("turn", 1, 1, 1), ("add2", 1, 1), ("add", 1, 1, 3),
     ("swap", 0, 0), ("swap", 1, 0), ("swap", 0, 1), ("swap", 1, 1),
 )
 
@@ -47,9 +47,9 @@
 
 def encoding_rows(shape, y, z):
     row = iota(shape, 0)
-    kk = row // (ROWS // 2)
-    first = (row // (4 * GROUP)) % 4
-    spot = (row // GROUP) % 4
+    kk = row // 16
+    first = (row // 4) % 4
+    spot = row % 4
     second = jnp.where(spot == 0, 2, jnp.where(spot == 1, 1, jnp.where(spot == 2, 3, 0)))
     dy = jnp.where(kk == 0, first, second)
     dz = jnp.where(kk == 0, second, first)
@@ -72,6 +72,12 @@
         step = 1 if direction == 0 else 3
         along_y = (kk == 0) == (stage == 1)
         return at_shot(step, 0) if along_y else at_shot(0, step)
+
+    barrier = pltpu.get_barrier_semaphore()
+    for peer in (at_shot(1, 0), at_shot(3, 0), at_shot(0, 1), at_shot(0, 3)):
+        pl.semaphore_signal(barrier, inc=1, device_id=peer, device_id_type=MESH)
+    for off in range(1, BLOCKS):
+        pl.semaphore_signal(barrier, inc=1, device_id=(shot, (rcv + off) % BLOCKS), device_id_type=MESH)
 
     loads = [pltpu.make_async_copy(code_hbm, codebuf, load_sem.at[0])]
     for chunk in range(4):
@@ -84,34 +90,28 @@
     for load in loads:
         load.start()
 
-    barrier = pltpu.get_barrier_semaphore()
-    for peer in (at_shot(1, 0), at_shot(3, 0), at_shot(0, 1), at_shot(0, 3)):
-        pl.semaphore_signal(barrier, inc=1, device_id=peer, device_id_type=MESH)
-    for off in range(1, BLOCKS):
-        pl.semaphore_signal(barrier, inc=1, device_id=(shot, (rcv + off) % BLOCKS), device_id_type=MESH)
-
+    pick = (encoding_rows((SUPERS, SUPERS), y, z) == iota((SUPERS, SUPERS), 1)).astype(BF16)
+    widen = (iota((SHOTS_DEV, DEPTH), 1) // GROUP == iota((SHOTS_DEV, DEPTH), 0)).astype(BF16)
+    same = iota((1, GROUP, DEPTH), 1) == iota((1, GROUP, DEPTH), 2) % GROUP
     loads[0].wait()
-    pick = (encoding_rows((ROWS, SUPERS), y, z) == iota((ROWS, SUPERS), 1)).astype(BF16)
     codes = jnp.dot(pick, codebuf[...].astype(F32).astype(BF16), preferred_element_type=F32).astype(BF16)
-    widen = (iota((SHOTS_DEV, DEPTH), 1) // GROUP == iota((SHOTS_DEV, DEPTH), 0)).astype(BF16)
     wide = jnp.dot(codes, widen, preferred_element_type=F32)
-    same = iota((ROWS, DEPTH), 0) % GROUP == iota((ROWS, DEPTH), 1) % GROUP
-    enc[...] = jnp.where(same, wide, 0.0).astype(BF16)
+    enc[...] = jnp.where(same, wide[:, None, :], 0.0).astype(BF16).reshape(ROWS, DEPTH)
 
     def half_rows(half):
         return pl.ds(half * HALF, HALF)
 
-    def encode(half, chunk):
-        def body(step, carry):
-            r0 = pl.multiple_of(chunk * 64 + step * GROUP, GROUP)
-            data = xbuf[:, pl.ds(r0, GROUP), :].reshape(DEPTH, SAMPLES)
+    def encode(chunk):
+        half = chunk // 2
+        for step in range(4):
+            r0 = chunk * 64 + step * GROUP
+            data = xbuf[:, r0:r0 + GROUP, :].reshape(DEPTH, SAMPLES)
+            rows, inner = pl.ds(r0, GROUP), pl.ds(r0 - half * HALF, GROUP)
             for kk in range(2):
                 product = jnp.dot(enc[kk * 256:(kk + 1) * 256, :], data, preferred_element_type=F32)
                 product = product.reshape(4, 4, GROUP, SAMPLES)
                 for th in range(2):
                     part = product[:, :, :, th * LANES:(th + 1) * LANES]
-                    rows = pl.ds(r0, GROUP)
-                    inner = pl.ds(pl.multiple_of(r0 - half * HALF, GROUP), GROUP)
                     own[kk, th, :, rows, :] = part[0]
                     send1[kk, th, 1, :, rows, :] = part[2].astype(BF16)
                     if half == 0:
@@ -120,11 +120,8 @@
                     else:
                         send1[kk, th, 0, :, rows, :] = part[1].astype(BF16)
                         keep[kk, th, 1, :, inner, :] = part[3]
-            return carry
-
-        lax.fori_loop(0, 4, body, 0, unroll=True)
-
-    def copy1(kk, th, kind, direction, spot):
+
+    def copy1(kk, th, kind, direction, spot, part_at=None):
         unit = 2 * kk + th
         slot = 1 if kind == 0 else (0 if direction == 0 else 2)
         half = direction if kind in (0, 2) else 1 - direction
@@ -134,8 +131,11 @@
             place, sems = got_turn.at[unit * 3 + spot, 2 * (kind - 1) + direction], (s_turn, r_turn.at[unit * 3 + spot])
         else:
             place, sems = got_last.at[unit, 2 * (kind - 1) + direction], (s_last, r_last.at[unit])
+        rows = half_rows(half)
+        if part_at is not None:
+            rows, place = pl.ds(half * HALF + part_at * 64, 64), place.at[pl.ds(part_at * 64, 64)]
         return pltpu.make_async_remote_copy(
-            src_ref=send1.at[kk, th, slot, spot, half_rows(half)],
+            src_ref=send1.at[kk, th, slot, spot, rows],
             dst_ref=place,
             send_sem=sems[0],
             recv_sem=sems[1],
@@ -174,13 +174,13 @@
     def arrived(place, sem):
         pltpu.make_async_copy(place, place, sem).wait()
 
-    def relay(kk, th, spot, directions=(0, 1)):
+    def relay(kk, th, spot, directions=(0, 1), part_at=None):
         for direction in directions:
-            copy1(kk, th, 0, direction, spot).start()
-
-    def plain(kk, th, spot, directions=(0, 1)):
+            copy1(kk, th, 0, direction, spot, part_at).start()
+
+    def plain(kk, th, spot, directions=(0, 1), part_at=None):
         for direction in directions:
-            copy1(kk, th, 1, direction, spot).start()
+            copy1(kk, th, 1, direction, spot, part_at).start()
 
     def add(kk, th, spot):
         at = (2 * kk + th) * 4 + spot
@@ -277,22 +277,17 @@
                 inj[...], jnp.concatenate(chosen, axis=1), (((1,), (1,)), ((), ())), preferred_element_type=F32
             ).astype(BF16)
 
-    loads[1].wait()
-    encode(0, 0)
-    loads[2].wait()
-    encode(0, 1)
-    pl.semaphore_wait(barrier, 4 + BLOCKS - 1)
-    for spot in range(4):
-        for kk in range(2):
-            relay(kk, 0, spot, (0,))
-    for spot in range(2):
-        for kk in range(2):
-            plain(kk, 0, spot, (1,))
-    loads[3].wait()
-    encode(1, 2)
-    loads[4].wait()
-    encode(1, 3)
-    for spot in range(4):
+    for chunk in range(4):
+        loads[1 + chunk].wait()
+        encode(chunk)
+        if chunk == 0:
+            pl.semaphore_wait(barrier, 4 + BLOCKS - 1)
+        for spot in range(4 if chunk < 2 else 2):
+            for kk in range(2):
+                relay(kk, 0, spot, (chunk // 2,), chunk % 2)
+                if chunk < 2 and spot < 3:
+                    plain(kk, 0, spot, (1,), chunk)
+    for spot in range(2, 4):
         for kk in range(2):
             relay(kk, 0, spot, (1,))
 
@@ -302,11 +297,11 @@
         if name not in ("relay", "plain") and not waiting:
             tables()
             waiting = True
-        if name == "plain" and th == 0 and spot[0] < 2:
+        if name == "plain" and th == 0 and spot[0] < 3:
             plain(kk, 0, spot[0], (0,))
         else:
             steps[name](kk, th, *spot)
-    for name, kk, th in SCHEDULE[-4:]:
+    for name, kk, th in [step for step in SCHEDULE if step[0] == "swap"]:
         inject(kk, th)
     arrived(got_relay, s_relay)
     arrived(got_turn, s_turn)

time: 37.2 us -> 36.6 us (0.984)
  Pallas kernels: 36.2 us -> 35.7 us
    pallas_call x1, Pallas kernels: 36.2 us -> 35.7 us  [local(): pl.pallas_call(kernel, out_shape=jax.ShapeDtypeStruct((2, GRID, SAMPLES),...]
where the time goes in v3:
time: 36.6 us; the launch traced here: 36.5 us
  Pallas kernels  35.7 us (98%)
  local copies, waits for them, and re-layouts  0.8 us (2%)
    pallas_call x1, Pallas kernels, local(): pl.pallas_call(kernel, out_shape=jax.ShapeDtypeStruct((2, GRID, SAMPLES),...  35.7 us
    unnamed x1, local copies, waits for them, and re-layouts  0.8 us

profile of v3, /device:TPU:1, one launch (start us, length us, event | category | flops | bytes accessed | tf_op | source)
XLA Modules:
  0.0 36.5 jit_solution(2382600071119752241)
XLA Ops:
  0.0 35.7 %shard_map.64 = f32[2,256,256]{2,1,0:T(8,128)S(1)} custom-call(bf16[32,256,256]{2,1,0:T(8,128)(2,1)} %shot_hbm.1, s32[32,32]{1,0:T(8,128)} %code_hbm.1, bf16[2,256,256]{2,1,0:T(8,128)(2,1)} %obs_hbm.1, s32[1,2048]{1,0:T(1,128)} %bitcast.5, s32[4,2048]{1,0:T(4,128)} %bitcast.3, f32[4,2048]{1,0:T(4,128)} %bitcast.4), custom_call_target="tpu_custom_call" | custom-call | tf_op jit(solution)/shard_map/pallas_call | solution.py:316
  35.7 0.8 %copy.8 = f32[2,256,256]{2,1,0:T(8,128)} copy(f32[2,256,256]{2,1,0:T(8,128)S(1)} %shard_map.64) | data formatting | bytes 1048576

commit v4 on v3

--- a/solution.py
+++ b/solution.py
@@ -58,7 +58,7 @@
 
 def kernel(
     shot_hbm, code_hbm, obs_hbm, blk_hbm, idx_hbm, wgt_hbm, out,
-    xbuf, codebuf, obsbuf, blk, idx, wgt, enc, inj, injc, sel,
+    xbuf, codebuf, obsbuf, blk, idx, wgt, wide, enc, inj, injc, sel,
     own, keep, send1, send2, send3, got_relay, got_turn, got_last, got_relay2, got_swap,
     load_sem, s_relay, s_turn, s_last, s_relay2, s_swap, r_relay, r_turn, r_last, r_relay2, r_swap,
 ):
@@ -87,16 +87,19 @@
     loads.append(pltpu.make_async_copy(blk_hbm, blk, load_sem.at[6]))
     loads.append(pltpu.make_async_copy(idx_hbm, idx, load_sem.at[7]))
     loads.append(pltpu.make_async_copy(wgt_hbm, wgt, load_sem.at[8]))
-    for load in loads:
+    for load in loads[:2]:
         load.start()
 
     pick = (encoding_rows((SUPERS, SUPERS), y, z) == iota((SUPERS, SUPERS), 1)).astype(BF16)
     widen = (iota((SHOTS_DEV, DEPTH), 1) // GROUP == iota((SHOTS_DEV, DEPTH), 0)).astype(BF16)
-    same = iota((1, GROUP, DEPTH), 1) == iota((1, GROUP, DEPTH), 2) % GROUP
+    same = iota((GROUP, DEPTH), 0) == iota((GROUP, DEPTH), 1) % GROUP
     loads[0].wait()
+    for load in loads[2:]:
+        load.start()
     codes = jnp.dot(pick, codebuf[...].astype(F32).astype(BF16), preferred_element_type=F32).astype(BF16)
-    wide = jnp.dot(codes, widen, preferred_element_type=F32)
-    enc[...] = jnp.where(same, wide[:, None, :], 0.0).astype(BF16).reshape(ROWS, DEPTH)
+    wide[...] = jnp.dot(codes, widen, preferred_element_type=F32)
+    for row in range(SUPERS):
+        enc[row * GROUP:(row + 1) * GROUP, :] = jnp.where(same, wide[row:row + 1, :], 0.0).astype(BF16)
 
     def half_rows(half):
         return pl.ds(half * HALF, HALF)
@@ -160,8 +163,11 @@
             device_id_type=MESH,
         )
 
+    def ranked(index):
+        return jnp.where(index < 4, index, jnp.where(index < 6, index + 2, index - 2))
+
     def copy3(kk, th, off):
-        block = (rcv + off) % BLOCKS
+        block = ranked(jnp.where(off <= ranked(rcv), off - 1, off))
         return pltpu.make_async_remote_copy(
             src_ref=send3.at[kk, th, pl.ds(pl.multiple_of(block * CAP, CAP), CAP)],
             dst_ref=got_swap.at[2 * kk + th, pl.ds(pl.multiple_of(rcv * CAP, CAP), CAP)],
@@ -236,7 +242,7 @@
         residual = jnp.concatenate(sums, axis=0)
         packed = jnp.dot(sel[...], residual, preferred_element_type=F32).astype(BF16)
         send3[kk, th] = packed
-        for off in (4, 3, 5, 2, 6, 1, 7):
+        for off in range(1, BLOCKS):
             copy3(kk, th, off).start()
         here = pl.ds(pl.multiple_of(rcv * CAP, CAP), CAP)
         got_swap[unit, here, :] = send3[kk, th, here, :]
@@ -325,6 +331,7 @@
             pltpu.VMEM((1, BLOCKS * RCV), I32),
             pltpu.VMEM((STENCIL, BLOCKS * RCV), I32),
             pltpu.VMEM((STENCIL, BLOCKS * RCV), F32),
+            pltpu.VMEM((SUPERS, DEPTH), F32),
             pltpu.VMEM((ROWS, DEPTH), BF16),
             pltpu.VMEM((GRID, 2 * RCV), BF16),
             pltpu.VMEM((GRID, BLOCKS * CAP), BF16),

time: 36.6 us -> 36.6 us (level)
  no operation moved by 1% of the time
where the time goes in v4:
time: 36.6 us; the launch traced here: 36.4 us
  Pallas kernels  35.6 us (97%)
  local copies, waits for them, and re-layouts  0.8 us (2%)
    pallas_call x1, Pallas kernels, local(): pl.pallas_call(kernel, out_shape=jax.ShapeDtypeStruct((2, GRID, SAMPLES),...  35.6 us
    unnamed x1, local copies, waits for them, and re-layouts  0.8 us

profile of v4, /device:TPU:1, one launch (start us, length us, event | category | flops | bytes accessed | tf_op | source)
XLA Modules:
  0.0 36.4 jit_solution(11907839133612147966)
XLA Ops:
  0.0 35.6 %shard_map.64 = f32[2,256,256]{2,1,0:T(8,128)S(1)} custom-call(bf16[32,256,256]{2,1,0:T(8,128)(2,1)} %shot_hbm.1, s32[32,32]{1,0:T(8,128)} %code_hbm.1, bf16[2,256,256]{2,1,0:T(8,128)(2,1)} %obs_hbm.1, s32[1,2048]{1,0:T(1,128)} %bitcast.5, s32[4,2048]{1,0:T(4,128)} %bitcast.3, f32[4,2048]{1,0:T(4,128)} %bitcast.4), custom_call_target="tpu_custom_call" | custom-call | tf_op jit(solution)/shard_map/pallas_call | solution.py:322
  35.6 0.8 %copy.8 = f32[2,256,256]{2,1,0:T(8,128)} copy(f32[2,256,256]{2,1,0:T(8,128)S(1)} %shard_map.64) | data formatting | bytes 1048576

commit v5 on v4

--- a/solution.py
+++ b/solution.py
@@ -87,15 +87,13 @@
     loads.append(pltpu.make_async_copy(blk_hbm, blk, load_sem.at[6]))
     loads.append(pltpu.make_async_copy(idx_hbm, idx, load_sem.at[7]))
     loads.append(pltpu.make_async_copy(wgt_hbm, wgt, load_sem.at[8]))
-    for load in loads[:2]:
+    for load in loads:
         load.start()
 
     pick = (encoding_rows((SUPERS, SUPERS), y, z) == iota((SUPERS, SUPERS), 1)).astype(BF16)
     widen = (iota((SHOTS_DEV, DEPTH), 1) // GROUP == iota((SHOTS_DEV, DEPTH), 0)).astype(BF16)
     same = iota((GROUP, DEPTH), 0) == iota((GROUP, DEPTH), 1) % GROUP
     loads[0].wait()
-    for load in loads[2:]:
-        load.start()
     codes = jnp.dot(pick, codebuf[...].astype(F32).astype(BF16), preferred_element_type=F32).astype(BF16)
     wide[...] = jnp.dot(codes, widen, preferred_element_type=F32)
     for row in range(SUPERS):
@@ -163,13 +161,10 @@
             device_id_type=MESH,
         )
 
-    def ranked(index):
-        return jnp.where(index < 4, index, jnp.where(index < 6, index + 2, index - 2))
-
     def copy3(kk, th, off):
-        block = ranked(jnp.where(off <= ranked(rcv), off - 1, off))
+        block = (rcv + off) % BLOCKS
         return pltpu.make_async_remote_copy(
-            src_ref=send3.at[kk, th, pl.ds(pl.multiple_of(block * CAP, CAP), CAP)],
+            src_ref=send3.at[kk, th, pl.ds(off * CAP, CAP)],
             dst_ref=got_swap.at[2 * kk + th, pl.ds(pl.multiple_of(rcv * CAP, CAP), CAP)],
             send_sem=s_swap,
             recv_sem=r_swap.at[2 * kk + th],
@@ -240,12 +235,14 @@
             seen = obsbuf[kk, half_rows(half), th * LANES:(th + 1) * LANES].astype(F32)
             sums[half] = (total - seen).astype(BF16)
         residual = jnp.concatenate(sums, axis=0)
-        packed = jnp.dot(sel[...], residual, preferred_element_type=F32).astype(BF16)
-        send3[kk, th] = packed
-        for off in range(1, BLOCKS):
-            copy3(kk, th, off).start()
+        for first, count in ((3, 3), (0, 3), (6, 2)):
+            rows = pl.ds(first * CAP, count * CAP)
+            send3[kk, th, rows, :] = jnp.dot(sel[rows, :], residual, preferred_element_type=F32).astype(BF16)
+            for off in range(first, first + count):
+                if off > 0:
+                    copy3(kk, th, off).start()
         here = pl.ds(pl.multiple_of(rcv * CAP, CAP), CAP)
-        got_swap[unit, here, :] = send3[kk, th, here, :]
+        got_swap[unit, here, :] = send3[kk, th, 0:CAP, :]
 
     def inject(kk, th):
         unit = 2 * kk + th
@@ -265,7 +262,9 @@
             return jnp.sum(named * count, axis=0, keepdims=True).astype(I32)
 
         mine = blk[:, pl.ds(pl.multiple_of(rcv * RCV, RCV), RCV)]
-        sel[...] = (iota((BLOCKS * CAP, RCV), 0) == mine * CAP + rank_of(mine)).astype(BF16)
+        sel[...] = (
+            iota((BLOCKS * CAP, RCV), 0) == (mine - rcv + BLOCKS) % BLOCKS * CAP + rank_of(mine)
+        ).astype(BF16)
         for pair in range(BLOCKS // 2):
             chosen = []
             for side in range(2):

time: 36.6 us -> 36.7 us (level)
  no operation moved by 1% of the time
where the time goes in v5:
time: 36.7 us; the launch traced here: 36.6 us
  Pallas kernels  35.7 us (97%)
  local copies, waits for them, and re-layouts  0.8 us (2%)
    pallas_call x1, Pallas kernels, local(): pl.pallas_call(kernel, out_shape=jax.ShapeDtypeStruct((2, GRID, SAMPLES),...  35.7 us
    unnamed x1, local copies, waits for them, and re-layouts  0.8 us

profile of v5, /device:TPU:1, one launch (start us, length us, event | category | flops | bytes accessed | tf_op | source)
XLA Modules:
  0.0 36.6 jit_solution(14848543205071863211)
XLA Ops:
  0.0 35.7 %shard_map.64 = f32[2,256,256]{2,1,0:T(8,128)S(1)} custom-call(bf16[32,256,256]{2,1,0:T(8,128)(2,1)} %shot_hbm.1, s32[32,32]{1,0:T(8,128)} %code_hbm.1, bf16[2,256,256]{2,1,0:T(8,128)(2,1)} %obs_hbm.1, s32[1,2048]{1,0:T(1,128)} %bitcast.5, s32[4,2048]{1,0:T(4,128)} %bitcast.3, f32[4,2048]{1,0:T(4,128)} %bitcast.4), custom_call_target="tpu_custom_call" | custom-call | tf_op jit(solution)/shard_map/pallas_call | solution.py:321
  35.8 0.8 %copy.8 = f32[2,256,256]{2,1,0:T(8,128)} copy(f32[2,256,256]{2,1,0:T(8,128)S(1)} %shard_map.64) | data formatting | bytes 1048576
